TPU v7x, 32 devices: a whole 2x2x4 slice. The times are simulated.
32 devices in a mesh: depth: 4 (over z), row: 2 (over x), col: 4 (over y, core).
Axes of the slice: x: 2, y: 2, z: 4, core: 2. Of those that a mesh axis runs over, the one named last changes fastest.
Arguments:
- tokens: bfloat16 [192, 8192], P('row', ('depth', 'col')), may hold values from -6 to 6
- cotangent: bfloat16 [192, 8192], P('row', ('depth', 'col')), may hold values from -1.609375 to 1.609375
- gate_weight: bfloat16 [8192, 14336], P(('depth', 'col'), 'row'), may hold values from -0.0625 to 0.0625
- up_weight: bfloat16 [8192, 14336], P(('depth', 'col'), 'row'), may hold values from -0.0625 to 0.0625
- down_weight: bfloat16 [14336, 8192], P('row', ('depth', 'col')), may hold values from -0.046875 to 0.046875
Outputs:
- input_grad: bfloat16 [192, 8192], P('row', ('depth', 'col'))
- gate_grad: bfloat16 [8192, 14336], P(('depth', 'col'), 'row')
- up_grad: bfloat16 [8192, 14336], P(('depth', 'col'), 'row')
- down_grad: bfloat16 [14336, 8192], P('row', ('depth', 'col'))
All inputs are finite; a program needn't handle non-finite values.
Results may differ from a plain program's by a relative error of at most 0.0065.
Values may be sent and summed in bfloat16 or wider, within the bound.
No kernel may reach another device: no remote copies, remote signals or barrier semaphores. Data moves between devices by JAX's collectives and lax.ppermute only.
A program may use at most 128 MiB of HBM per device.

v0:
```python
import jax
import jax.numpy as jnp
from jax import lax
from jax.sharding import PartitionSpec as P


def swiglu_back(gate, up, back):
    sig = jax.nn.sigmoid(gate)
    hidden = (gate * sig * up).astype(jnp.bfloat16)
    grad_gate = (back * up * sig * (1.0 + gate * (1.0 - sig))).astype(jnp.bfloat16)
    grad_up = (back * gate * sig).astype(jnp.bfloat16)
    return (hidden, grad_gate, grad_up)


def contract_rows(left, right):
    return lax.dot_general(
        left, right, (((0,), (0,)), ((), ())), preferred_element_type=jnp.float32
    )


def contract_cols(left, right):
    return lax.dot_general(
        left, right, (((1,), (1,)), ((), ())), preferred_element_type=jnp.float32
    )


def stationary(tokens, cotangent, gate_weight, up_weight, down_weight):
    rows_all, cot_all = (
        lax.all_gather(tokens, "row", axis=0, tiled=True),
        lax.all_gather(cotangent, "row", axis=0, tiled=True),
    )
    width = gate_weight.shape[1]
    rows_part = rows_all
    cot_part = cot_all
    gate_part = jnp.dot(rows_part, gate_weight, preferred_element_type=jnp.float32)
    up_part = jnp.dot(rows_part, up_weight, preferred_element_type=jnp.float32)
    back_part = contract_cols(cot_part, down_weight)
    summed = lax.psum_scatter(
        jnp.concatenate([gate_part, up_part, back_part], axis=1),
        ("depth", "col"),
        scatter_dimension=0,
        tiled=True,
    )
    hidden, grad_gate, grad_up = swiglu_back(
        summed[:, :width], summed[:, width : 2 * width], summed[:, 2 * width :]
    )
    hidden_piece = lax.all_gather(hidden, ("depth", "col"), axis=0, tiled=True)
    gate_piece = lax.all_gather(grad_gate, ("depth", "col"), axis=0, tiled=True)
    up_piece = lax.all_gather(grad_up, ("depth", "col"), axis=0, tiled=True)
    rows_part = rows_all
    cot_part = cot_all
    acc_gate = contract_rows(rows_part, gate_piece)
    acc_up = contract_rows(rows_part, up_piece)
    acc_down = contract_rows(hidden_piece, cot_part)
    block = contract_cols(gate_piece, gate_weight) + contract_cols(up_piece, up_weight)
    input_grad = lax.psum_scatter(block, "row", scatter_dimension=0, tiled=True).astype(
        jnp.bfloat16
    )
    return (
        input_grad,
        acc_gate.astype(jnp.bfloat16),
        acc_up.astype(jnp.bfloat16),
        acc_down.astype(jnp.bfloat16),
    )


def on_device(tokens, cotangent, gate_weight, up_weight, down_weight):
    return stationary(tokens, cotangent, gate_weight, up_weight, down_weight)


def solution(mesh):
    return jax.shard_map(
        on_device,
        mesh=mesh,
        in_specs=(
            P("row", ("depth", "col")),
            P("row", ("depth", "col")),
            P(("depth", "col"), "row"),
            P(("depth", "col"), "row"),
            P("row", ("depth", "col")),
        ),
        out_specs=(
            P("row", ("depth", "col")),
            P(("depth", "col"), "row"),
            P(("depth", "col"), "row"),
            P("row", ("depth", "col")),
        ),
        check_vma=False,
    )
```

profile of v0, /device:TPU:0, one launch (start us, length us, event | category | flops | bytes accessed | tf_op | source)
XLA Modules:
  0.0 501.4 jit_solution(8831859143707906585)
XLA Ops:
  7.2 0.0 slice-start
  7.2 0.0 all-reduce.3.cloned.1.call-start
  7.2 6.8 %all_gather.15 = bf16[192,512]{1,0:T(8,128)(2,1)S(1)} all-gather(bf16[96,512]{1,0:T(8,128)(2,1)} %param.5), channel_id=1, replica_groups=mesh['depth'=4,'row'=2,'col'=4] {'row'}, dimensions={0}, use_global_device_ids=true | all-gather | bytes 294912 | tf_op jit(solution)/shard_map/all_gather | solution.py:29
  14.0 0.0 slice-start.1
  14.0 4.8 fusion.5
  18.9 0.0 slice-done
  18.9 0.0 slice-done.1
  18.9 0.0 copy-start.1
  18.9 1.6 fusion.6
  20.5 0.0 copy-done.1
  20.5 5.3 %all_gather.16 = bf16[192,512]{1,0:T(8,128)(2,1)S(1)} all-gather(bf16[96,512]{1,0:T(8,128)(2,1)S(1)} %copy-done.1), channel_id=1, replica_groups=mesh['depth'=4,'row'=2,'col'=4] {'row'}, dimensions={0}, use_global_device_ids=true | all-gather | bytes 294912 | tf_op jit(solution)/shard_map/all_gather | solution.py:30
  25.8 5.6 %fusion.7 = f32[192,7168]{1,0:T(8,128)S(1)} fusion(bf16[192,512]{1,0:T(8,128)(2,1)S(1)} %all_gather.16, bf16[7168,512]{1,0:T(8,128)(2,1)} %param.9), kind=kOutput, calls=%fused_computation.16 | convolution fusion | flops 1409286144 | bytes 13041664 | tf_op jit(solution)/shard_map/dot_general | solution.py:22
  31.4 6.0 %pad_maximum_fusion = f32[192,21504]{1,0:T(8,128)} fusion(f32[192,7168]{1,0:T(8,128)S(1)} %fusion.7, f32[192,7168]{1,0:T(8,128)S(1)} %fusion.6, f32[192,7168]{1,0:T(8,128)S(1)} %fusion.5), kind=kLoop, calls=%fused_computation | loop fusion | flops 8257536 | bytes 33030144 | tf_op jit(solution)/shard_map/concatenate | solution.py:39
  37.4 0.0 copy-start.2
  37.4 0.0 all-reduce.3.cloned.1.call-update
  37.4 0.0 all-gather.7.cloned.1.call-start
  37.4 0.6 copy-done.2
  38.0 0.6 dynamic-slice
  39.2 292.3 %all-reduce.3.cloned.1.call-done = f32[192,21504]{1,0:T(8,128)} async-done(((f32[192,21504]{1,0:T(8,128)}), f32[192,21504]{1,0:T(8,128)}) %all-reduce.3.cloned.1.call-update) | async-done | bytes 16515088
  331.5 2.7 fusion.3
  334.2 0.0 all-gather.7.cloned.1.call-update
  334.3 0.0 all-gather.9.cloned.1.call-start
  334.3 0.7 all-gather.9.cloned.1.call-update
  335.0 0.0 all-gather.11.cloned.1.call-start
  335.0 0.5 all-gather.11.cloned.1.call-update
  335.6 0.2 reduce-scatter.2.cloned.1.call-start
  335.8 46.3 %all-gather.7.cloned.1.call-done = bf16[16,12,7168]{2,1,0:T(8,128)(2,1)} async-done(((bf16[1,12,7168]{2,1,0:T(8,128)(2,1)}), bf16[16,12,7168]{2,1,0:T(8,128)(2,1)}) %all-gather.7.cloned.1.call-update) | async-done | bytes 2752528 | tf_op jit(solution)/shard_map/all_gather | solution.py:48
  382.1 3.0 reshape.9
  385.2 0.0 copy-start
  385.2 5.2 %fusion = bf16[512,7168]{0,1:T(8,128)(2,1)} fusion(bf16[192,7168]{1,0:T(8,128)(2,1)S(1)} %reshape.9, bf16[192,512]{1,0:T(8,128)(2,1)S(1)} %all_gather.15), kind=kOutput, calls=%fused_computation.4 | convolution fusion | flops 1412956160 | bytes 10289152 | tf_op jit(solution)/shard_map/dot_general | solution.py:16
  390.3 10.0 %copy.13 = bf16[512,7168]{1,0:T(8,128)(2,1)} copy(bf16[512,7168]{0,1:T(8,128)(2,1)} %fusion) | data formatting | bytes 14680064
  400.3 0.0 copy-done
  400.3 30.5 %all-gather.9.cloned.1.call-done = bf16[16,12,7168]{2,1,0:T(8,128)(2,1)} async-done(((bf16[1,12,7168]{2,1,0:T(8,128)(2,1)}), bf16[16,12,7168]{2,1,0:T(8,128)(2,1)}) %all-gather.9.cloned.1.call-update) | async-done | bytes 2752528 | tf_op jit(solution)/shard_map/all_gather | solution.py:49
  430.8 3.0 reshape.11
  433.8 6.5 %fusion.8 = f32[192,512]{1,0:T(8,128)S(1)} fusion(bf16[192,7168]{1,0:T(8,128)(2,1)} %copy-done, bf16[512,7168]{1,0:T(8,128)(2,1)} %param.7), kind=kOutput, calls=%fused_computation.17 | convolution fusion | flops 1409286144 | bytes 10485760 | tf_op jit(solution)/shard_map/dot_general | solution.py:22
  440.3 6.4 %convolution_add_fusion = f32[192,512]{1,0:T(8,128)} fusion(f32[192,512]{1,0:T(8,128)S(1)} %fusion.8, bf16[192,7168]{1,0:T(8,128)(2,1)S(1)} %reshape.11, bf16[512,7168]{1,0:T(8,128)(2,1)} %param.8), kind=kOutput, calls=%fused_computation.6 | convolution fusion | flops 1409384448 | bytes 10878976 | tf_op jit(solution)/shard_map/dot_general | solution.py:22
  446.7 0.0 reduce-scatter.2.cloned.1.call-update
  446.7 5.2 %fusion.1 = bf16[512,7168]{0,1:T(8,128)(2,1)} fusion(bf16[192,7168]{1,0:T(8,128)(2,1)S(1)} %reshape.11, bf16[192,512]{1,0:T(8,128)(2,1)S(1)} %all_gather.15), kind=kOutput, calls=%fused_computation.5 | convolution fusion | flops 1412956160 | bytes 10289152 | tf_op jit(solution)/shard_map/dot_general | solution.py:16
  451.9 10.0 %copy.14 = bf16[512,7168]{1,0:T(8,128)(2,1)} copy(bf16[512,7168]{0,1:T(8,128)(2,1)} %fusion.1) | data formatting | bytes 14680064
  461.9 17.4 %all-gather.11.cloned.1.call-done = bf16[16,12,7168]{2,1,0:T(8,128)(2,1)} async-done(((bf16[1,12,7168]{2,1,0:T(8,128)(2,1)}), bf16[16,12,7168]{2,1,0:T(8,128)(2,1)}) %all-gather.11.cloned.1.call-update) | async-done | bytes 2752528 | tf_op jit(solution)/shard_map/all_gather | solution.py:47
  479.3 3.0 reshape.13
  482.4 5.2 %convolution_convert_fusion = bf16[7168,512]{1,0:T(8,128)(2,1)} fusion(bf16[192,7168]{1,0:T(8,128)(2,1)S(1)} %reshape.13, bf16[192,512]{1,0:T(8,128)(2,1)S(1)} %all_gather.16), kind=kOutput, calls=%fused_computation.1 | convolution fusion | flops 1412956160 | bytes 10289152 | tf_op jit(solution)/shard_map/dot_general | solution.py:16
  487.5 5.8 %reduce-scatter.2.cloned.1.call-done = f32[96,512]{1,0:T(8,128)} async-done(((f32[192,512]{1,0:T(8,128)}), f32[96,512]{1,0:T(8,128)}) %reduce-scatter.2.cloned.1.call-update) | async-done | bytes 196624 | tf_op jit(solution)/shard_map/reduce_scatter | solution.py:56
  493.3 1.6 convert_element_type.29
  (1 shorter events, 0.0 us)
Async XLA Ops:
  7.2 11.7 %slice-start = ((s8[7340032]{0:T(1024)(128)(4,1)}), s8[3145728]{0:T(1024)(128)(4,1)S(1)}, s32[]{:S(2)}) async-start(s8[7340032]{0:T(1024)(128)(4,1)} %bitcast.27), calls=%async_computation.6 | async-start | bytes 6291456
  7.2 324.3 %all-reduce.3.cloned.1.call-start = ((), (), s32[]{:S(2)}) async-start(), calls=%async_computation.5 | async-start | bytes 33030144
  14.0 4.9 slice-start.1
  18.9 1.6 copy-start.1
  37.4 0.7 copy-start.2
  37.4 344.7 %all-gather.7.cloned.1.call-start = ((), (), s32[]{:S(2)}) async-start(), calls=%async_computation.2 | async-start | bytes 3899392 | tf_op jit(solution)/shard_map/all_gather | solution.py:48
  334.3 96.5 %all-gather.9.cloned.1.call-start = ((), (), s32[]{:S(2)}) async-start(), calls=%async_computation.3 | async-start | bytes 3899392 | tf_op jit(solution)/shard_map/all_gather | solution.py:49
  335.0 144.3 %all-gather.11.cloned.1.call-start = ((), (), s32[]{:S(2)}) async-start(), calls=%async_computation.4 | async-start | bytes 3899392 | tf_op jit(solution)/shard_map/all_gather | solution.py:47
  335.6 157.8 %reduce-scatter.2.cloned.1.call-start = ((), (), s32[]{:S(2)}) async-start(), calls=%async_computation.1 | async-start | bytes 589824 | tf_op jit(solution)/shard_map/reduce_scatter | solution.py:56
  385.2 15.2 %copy-start = (bf16[192,7168]{1,0:T(8,128)(2,1)}, bf16[192,7168]{1,0:T(8,128)(2,1)S(1)}, u32[]{:S(2)}) copy-start(bf16[192,7168]{1,0:T(8,128)(2,1)S(1)} %reshape.9) | copy-start | bytes 8257540
Sparse Core Ops, SparseCore 0:
  37.5 293.9 all-reduce.2
  334.4 47.7 all-gather.6
  384.4 46.3 all-gather.8
  432.9 46.3 all-gather.10
  481.4 11.8 reduce-scatter.1
where the time goes:
time: 502 us; the launch traced here: 501 us
  waiting for transfers between devices  393 us (78%)
  matrix products  40.4 us (8%)
  local copies, waits for them, and re-layouts  30.3 us (6%)
  between operations  14.5 us (3%)
  blocking collectives  12.1 us (2%)
  other arithmetic  10.3 us (2%)
    unnamed x6, waiting for transfers between devices  294 us
    all_gather x1, waiting for transfers between devices, stationary(): gate_piece = lax.all_gather(grad_gate, ('depth', 'col'), axis=0, tiled=True)  46.3 us
    all_gather x1, waiting for transfers between devices, stationary(): up_piece = lax.all_gather(grad_up, ('depth', 'col'), axis=0, tiled=True)  30.5 us
    unnamed x16, local copies, waits for them, and re-layouts  30.3 us
    dot_general x3, matrix products, contract_cols(): lax.dot_general(left, right, (((1,), (1,)), ((), ())), preferred_element_...  18.5 us
    all_gather x1, waiting for transfers between devices, stationary(): hidden_piece = lax.all_gather(hidden, ('depth', 'col'), axis=0, tiled=True)  17.4 us
    dot_general x3, matrix products, contract_rows(): lax.dot_general(left, right, (((0,), (0,)), ((), ())), preferred_element_...  15.5 us
  transfers between devices with their start and end apart: 5, of which 5 were waited for; matrix products, arithmetic and copies ran while one was open for 12% of the time, Pallas kernels for 0%

commit v1 on v0

--- a/solution.py
+++ b/solution.py
@@ -44,8 +44,13 @@
     hidden, grad_gate, grad_up = swiglu_back(
         summed[:, :width], summed[:, width : 2 * width], summed[:, 2 * width :]
     )
-    hidden_piece = lax.all_gather(hidden, ("depth", "col"), axis=0, tiled=True)
-    gate_piece = lax.all_gather(grad_gate, ("depth", "col"), axis=0, tiled=True)
+    hidden_piece, gate_piece = jnp.split(
+        lax.all_gather(
+            jnp.concatenate([hidden, grad_gate], axis=1), ("depth", "col"), axis=0, tiled=True
+        ),
+        [hidden.shape[1]],
+        axis=1,
+    )
     up_piece = lax.all_gather(grad_up, ("depth", "col"), axis=0, tiled=True)
     rows_part = rows_all
     cot_part = cot_all

time: 502 us -> 497 us (0.990)
  waiting for transfers between devices: 393 us -> 385 us
    all_gather x2 -> x1, waiting for transfers between devices: 63.7 us -> 45.4 us  [stationary(): lax.all_gather(jnp.concatenate([hidden, grad_gate], axis=1), ('depth', 'c...]
    all_gather x1, waiting for transfers between devices: 30.5 us -> 46.9 us  [stationary(): up_piece = lax.all_gather(grad_up, ('depth', 'col'), axis=0, tiled=True)]
    reduce_scatter x1, waiting for transfers between devices: 5.8 us -> 0.01 us  [stationary(): lax.psum_scatter(block, 'row', scatter_dimension=0, tiled=True)]
    unnamed x16 -> x15, local copies, waits for them, and re-layouts: 30.3 us -> 32.5 us
    unnamed x6 -> x5, waiting for transfers between devices: 294 us -> 292 us
  transfers between devices with their start and end apart: 5 -> 4, of which waited for: 5 -> 3; matrix products, arithmetic and copies ran while one was open for 12% -> 10% of each run, Pallas kernels for 0% -> 0%
where the time goes in v1:
time: 497 us; the launch traced here: 496 us
  waiting for transfers between devices  385 us (77%)
  matrix products  41.2 us (8%)
  local copies, waits for them, and re-layouts  32.5 us (7%)
  between operations  14.5 us (3%)
  blocking collectives  12.1 us (2%)
  other arithmetic  10.9 us (2%)
    unnamed x5, waiting for transfers between devices  292 us
    all_gather x1, waiting for transfers between devices, stationary(): up_piece = lax.all_gather(grad_up, ('depth', 'col'), axis=0, tiled=True)  46.9 us
    all_gather x1, waiting for transfers between devices, stationary(): lax.all_gather(jnp.concatenate([hidden, grad_gate], axis=1), ('depth', 'c...  45.4 us
    unnamed x15, local copies, waits for them, and re-layouts  32.5 us
    dot_general x3, matrix products, contract_rows(): lax.dot_general(left, right, (((0,), (0,)), ((), ())), preferred_element_...  19.1 us
    dot_general x3, matrix products, contract_cols(): lax.dot_general(left, right, (((1,), (1,)), ((), ())), preferred_element_...  15.5 us
  transfers between devices with their start and end apart: 4, of which 3 were waited for; matrix products, arithmetic and copies ran while one was open for 10% of the time, Pallas kernels for 0%

profile of v1, /device:TPU:0, one launch (start us, length us, event | category | flops | bytes accessed | tf_op | source)
XLA Modules:
  0.0 496.1 jit_solution(1523845829363775441)
XLA Ops:
  7.2 0.0 all-reduce.3.cloned.1.call-start
  7.2 0.0 copy-start
  7.2 6.8 %all_gather.12 = bf16[192,512]{1,0:T(8,128)(2,1)S(1)} all-gather(bf16[96,512]{1,0:T(8,128)(2,1)} %param.5), channel_id=1, replica_groups=mesh['depth'=4,'row'=2,'col'=4] {'row'}, dimensions={0}, use_global_device_ids=true | all-gather | bytes 294912 | tf_op jit(solution)/shard_map/all_gather | solution.py:29
  14.0 0.0 slice-start
  14.0 4.8 fusion.10
  18.9 0.0 copy-done
  18.9 0.0 copy-start.1
  18.9 0.0 slice-start.1
  18.9 1.7 fusion.11
  20.6 0.0 copy-done.1
  20.6 5.3 %all_gather.13 = bf16[192,512]{1,0:T(8,128)(2,1)S(1)} all-gather(bf16[96,512]{1,0:T(8,128)(2,1)S(1)} %copy-done.1), channel_id=1, replica_groups=mesh['depth'=4,'row'=2,'col'=4] {'row'}, dimensions={0}, use_global_device_ids=true | all-gather | bytes 294912 | tf_op jit(solution)/shard_map/all_gather | solution.py:30
  25.9 0.0 slice-done
  25.9 0.0 slice-done.1
  25.9 2.6 fusion.12
  28.5 6.0 %pad_maximum_fusion = f32[192,21504]{1,0:T(8,128)} fusion(f32[192,7168]{1,0:T(8,128)S(1)} %fusion.12, f32[192,7168]{1,0:T(8,128)S(1)} %fusion.11, f32[192,7168]{1,0:T(8,128)S(1)} %fusion.10), kind=kLoop, calls=%fused_computation | loop fusion | flops 8257536 | bytes 33030144 | tf_op jit(solution)/shard_map/concatenate | solution.py:39
  34.5 0.0 copy-start.2
  34.5 0.0 all-reduce.3.cloned.1.call-update
  34.5 0.0 all-gather.7.cloned.1.call-start
  34.5 0.6 copy-done.2
  35.1 0.6 dynamic-slice
  36.4 292.3 %all-reduce.3.cloned.1.call-done = f32[192,21504]{1,0:T(8,128)} async-done(((f32[192,21504]{1,0:T(8,128)}), f32[192,21504]{1,0:T(8,128)}) %all-reduce.3.cloned.1.call-update) | async-done | bytes 16515088
  328.6 2.6 multiply_convert_fusion.2
  331.2 0.0 all-gather.7.cloned.1.call-update
  331.2 0.0 all-gather.5.cloned.1.call-start
  331.3 0.8 maximum_bitcast_fusion
  332.1 0.0 all-gather.5.cloned.1.call-update
  332.1 0.2 reduce-scatter.2.cloned.1.call-start
  332.3 46.9 %all-gather.7.cloned.1.call-done = bf16[16,12,7168]{2,1,0:T(8,128)(2,1)} async-done(((bf16[1,12,7168]{2,1,0:T(8,128)(2,1)}), bf16[16,12,7168]{2,1,0:T(8,128)(2,1)}) %all-gather.7.cloned.1.call-update) | async-done | bytes 2752528 | tf_op jit(solution)/shard_map/all_gather | solution.py:54
  379.2 3.0 reshape.11
  382.3 5.2 %fusion.1 = bf16[512,7168]{0,1:T(8,128)(2,1)} fusion(bf16[192,7168]{1,0:T(8,128)(2,1)S(1)} %reshape.11, bf16[192,512]{1,0:T(8,128)(2,1)S(1)} %all_gather.12), kind=kOutput, calls=%fused_computation.5 | convolution fusion | flops 1412956160 | bytes 10289152 | tf_op jit(solution)/shard_map/dot_general | solution.py:16
  387.4 10.0 %copy.14 = bf16[512,7168]{1,0:T(8,128)(2,1)} copy(bf16[512,7168]{0,1:T(8,128)(2,1)} %fusion.1) | data formatting | bytes 14680064
  397.4 5.7 %fusion.13 = f32[192,512]{1,0:T(8,128)S(1)} fusion(bf16[192,7168]{1,0:T(8,128)(2,1)S(1)} %reshape.11, bf16[512,7168]{1,0:T(8,128)(2,1)} %param.8), kind=kOutput, calls=%fused_computation.20 | convolution fusion | flops 1409286144 | bytes 10485760 | tf_op jit(solution)/shard_map/dot_general | solution.py:22
  403.1 45.4 %all-gather.5.cloned.1.call-done = bf16[16,12,14336]{2,1,0:T(8,128)(2,1)} async-done(((bf16[1,12,14336]{2,1,0:T(8,128)(2,1)}), bf16[16,12,14336]{2,1,0:T(8,128)(2,1)}) %all-gather.5.cloned.1.call-update) | async-done | bytes 5505040 | tf_op jit(solution)/shard_map/all_gather | solution.py:48
  448.5 8.3 %reshape.9 = bf16[192,14336]{1,0:T(8,128)(2,1)} reshape(bf16[16,12,14336]{2,1,0:T(8,128)(2,1)} %all-gather.5.cloned.1.call-done) | data formatting | bytes 11010048
  456.8 7.2 %fusion.6 = f32[192,512]{1,0:T(8,128)} fusion(f32[192,512]{1,0:T(8,128)S(1)} %fusion.13, bf16[512,7168]{1,0:T(8,128)(2,1)} %param.7, bf16[192,14336]{1,0:T(8,128)(2,1)} %reshape.9), kind=kOutput, calls=%fused_computation.10 | convolution fusion | flops 1409384448 | bytes 10878976 | tf_op jit(solution)/shard_map/dot_general | solution.py:22
  464.0 0.0 reduce-scatter.2.cloned.1.call-update
  464.1 7.0 %fusion = bf16[512,7168]{0,1:T(8,128)(2,1)} fusion(bf16[192,512]{1,0:T(8,128)(2,1)S(1)} %all_gather.12, bf16[192,14336]{1,0:T(8,128)(2,1)} %reshape.9), kind=kOutput, calls=%fused_computation.4 | convolution fusion | flops 1412956160 | bytes 10289152 | tf_op jit(solution)/shard_map/dot_general | solution.py:16
  471.1 9.9 %copy.13 = bf16[512,7168]{1,0:T(8,128)(2,1)} copy(bf16[512,7168]{0,1:T(8,128)(2,1)} %fusion) | data formatting | bytes 14680064
  481.0 7.0 %convolution_convert_fusion = bf16[7168,512]{1,0:T(8,128)(2,1)} fusion(bf16[192,512]{1,0:T(8,128)(2,1)S(1)} %all_gather.13, bf16[192,14336]{1,0:T(8,128)(2,1)} %reshape.9), kind=kOutput, calls=%fused_computation.1 | convolution fusion | flops 1412956160 | bytes 10289152 | tf_op jit(solution)/shard_map/dot_general | solution.py:16
  488.0 0.0 reduce-scatter.2.cloned.1.call-done
  488.0 1.6 convert_element_type.30
  (1 shorter events, 0.0 us)
Async XLA Ops:
  7.2 321.4 %all-reduce.3.cloned.1.call-start = ((), (), s32[]{:S(2)}) async-start(), calls=%async_computation.4 | async-start | bytes 33030144
  7.2 11.6 %copy-start = (bf16[512,7168]{1,0:T(8,128)(2,1)S(1)}, bf16[512,7168]{1,0:T(8,128)(2,1)}, u32[]{:S(2)}) copy-start(bf16[512,7168]{1,0:T(8,128)(2,1)} %param.8) | copy-start | bytes 22020100
  14.0 11.9 %slice-start = ((s8[7340032]{0:T(1024)(128)(4,1)}), s8[4194304]{0:T(1024)(128)(4,1)S(1)}, s32[]{:S(2)}) async-start(s8[7340032]{0:T(1024)(128)(4,1)} %bitcast.22), calls=%async_computation.5 | async-start | bytes 8388608
  18.9 1.8 copy-start.1
  18.9 7.1 %slice-start.1 = ((s8[7340032]{0:T(1024)(128)(4,1)}), s8[3145728]{0:T(1024)(128)(4,1)S(1)}, s32[]{:S(2)}) async-start(s8[7340032]{0:T(1024)(128)(4,1)} %bitcast.22), calls=%async_computation.6 | async-start | bytes 6291456
  34.5 0.7 copy-start.2
  34.5 344.7 %all-gather.7.cloned.1.call-start = ((), (), s32[]{:S(2)}) async-start(), calls=%async_computation.3 | async-start | bytes 3899392 | tf_op jit(solution)/shard_map/all_gather | solution.py:54
  331.2 117.3 %all-gather.5.cloned.1.call-start = ((), (), s32[]{:S(2)}) async-start(), calls=%async_computation.2 | async-start | bytes 7798784 | tf_op jit(solution)/shard_map/all_gather | solution.py:48
  332.1 155.9 %reduce-scatter.2.cloned.1.call-start = ((), (), s32[]{:S(2)}) async-start(), calls=%async_computation.1 | async-start | bytes 589824 | tf_op jit(solution)/shard_map/reduce_scatter | solution.py:61
Sparse Core Ops, SparseCore 0:
  34.6 293.9 all-reduce.2
  331.5 47.7 all-gather.6
  382.1 66.3 all-gather.4
  464.2 11.9 reduce-scatter.1
